TPU v7x, 32 devices: a whole 2x2x4 slice. The times are simulated.
32 devices in a mesh: ep: 8 (over z, y), tp: 4 (over x, core).
Axes of the slice: x: 2, y: 2, z: 4, core: 2. Of those that a mesh axis runs over, the one named last changes fastest.
Arguments:
- tokens: bfloat16 [4096, 2048], P(('ep', 'tp')), may hold values from -6 to 6
- norm_gain: float32 [2048], replicated, may hold values from 0.1 to 1.9
- expert_ids: int32 [4096, 6], P(('ep', 'tp')), may hold values from 0 to 15, as said below
- slot_index: int32 [4096, 6], P(('ep', 'tp')), may hold values from 0 to 63, as said below
- dropped: int32 [4096, 6], P(('ep', 'tp')), may hold values from 0 to 1, as said below
- gates: float32 [4096, 6], P(('ep', 'tp')), may hold values from 0.05 to 0.8
- w_gate: bfloat16 [16, 2048, 704], P('ep', None, 'tp'), may hold values from -0.125 to 0.125
- w_up: bfloat16 [16, 2048, 704], P('ep', None, 'tp'), may hold values from -0.125 to 0.125
- w_down: bfloat16 [16, 2048, 704], P('ep', None, 'tp'), may hold values from -0.21875 to 0.21875
- shared_gate: bfloat16 [2048, 1408], P(None, 'tp'), may hold values from -0.125 to 0.125
- shared_up: bfloat16 [2048, 1408], P(None, 'tp'), may hold values from -0.125 to 0.125
- shared_down: bfloat16 [1408, 2048], replicated, may hold values from -0.15625 to 0.15625
Outputs:
- layer_out: bfloat16 [4096, 2048], P(('ep', 'tp'))
Inputs may be any that keep to these rules, and one draw needn't show every extreme that they name: `expert_ids`: each token names 6 different experts; some expert has 64 kept pairs from the tokens of every device. `slot_index`: for a kept pair, its place among the slots of its expert for the tokens of its device (the tokens n with one value of n // 128); the kept pairs of one device and one expert have distinct places; 0 for a dropped pair. `dropped`: 1 for the pairs of a device and an expert beyond the 64 that are kept.
All inputs are finite; a program needn't handle non-finite values.
Results may differ from a plain program's by a relative error of at most 0.0054.
Values may be sent and summed in bfloat16 or wider, within the bound.
A program may use at most 128 MiB of HBM per device.

v0:
```python
import functools

import jax
import jax.numpy as jnp
from jax import lax
from jax.experimental import pallas as pl
from jax.experimental.pallas import tpu as pltpu
from jax.sharding import PartitionSpec as P

MESH = pl.DeviceIdType.MESH
CORES = 2
COLS = 2
VMEM_BYTES = 62 * 1024 * 1024
PIECES = 8

NT = (((1,), (1,)), ((), ()))
NN = (((1,), (0,)), ((), ()))


def dot(a, b, dims):
    return lax.dot_general(a, b, dims, preferred_element_type=jnp.float32)


def flip(index, mask, size):
    out, bit = 0, 1
    while bit < size:
        digit = (index // bit) % 2
        out = out + (1 - digit if mask & bit else digit) * bit
        bit *= 2
    return out


def layer_kernel(
    n_rows_z,
    tokens,
    gain,
    ids,
    dropped,
    gates,
    w_gate,
    w_up,
    w_down,
    s_gate,
    s_up,
    s_down,
    out,
    xb,
    wtb,
    gu,
    ga,
    db,
    hb,
    sb,
    sg,
    su,
    sd,
    sh,
    whid,
    ysend,
    yrecv,
    ypart,
    zsend,
    zrecv,
    w_send,
    w_recv,
    own_sem,
    z_send,
    z_recv,
    y_send,
    y_recv,
    t_send,
    t_recv,
    h_send,
    h_recv,
    ry_send,
    ry_recv,
    rz_send,
    rz_recv,
):
    ep, tp = lax.axis_index("ep"), lax.axis_index("tp")
    z, y = ep // COLS, ep % COLS
    x, core = tp // CORES, tp % CORES
    rows, width = tokens.shape
    experts = w_gate.shape[0]
    hid = w_gate.shape[1]
    shid = s_gate.shape[0]
    piece = width // PIECES
    mate = (ep, x * CORES + 1 - core)
    across = (ep, (1 - x) * CORES + core)
    diagonal = (ep, (1 - x) * CORES + 1 - core)
    beside = (z * COLS + 1 - y, tp)
    along = [None] + [(flip(z, r, n_rows_z) * COLS + y, tp) for r in range(1, n_rows_z)]

    barrier = pltpu.get_barrier_semaphore()
    peers = [mate, across, diagonal, beside] + along[1:]
    for peer in peers:
        pl.semaphore_signal(barrier, inc=1, device_id=peer, device_id_type=MESH)

    def local(src, dst, sem):
        c = pltpu.make_async_copy(src, dst, sem)
        c.start()
        return c

    own = []
    chunks = []
    for e in range(experts):
        for m, source in enumerate((w_gate, w_up)):
            chunks.append((source.at[e], functools.partial(lambda e, m, s: gu.at[e, m, s], e, m)))
    first_down = len(chunks)
    for c in range(PIECES):
        cut = pl.ds(c * piece, piece)
        chunks.append(
            (w_down.at[:, :, cut], functools.partial(lambda cut, s: db.at[:, s, :, cut], cut))
        )
    for k, (source, place) in enumerate(chunks):
        own.append(local(source, place(0), own_sem.at[k]))
    n = len(chunks)
    shared_in = [local(s_gate, sg, own_sem.at[n]), local(s_up, su, own_sem.at[n + 1])]
    who = [tp, mate[1], across[1], diagonal[1]]
    shared_down_in = [
        local(
            s_down.at[pl.ds(pl.multiple_of(who[s] * shid, 16), shid), :],
            sd.at[s],
            own_sem.at[n + 2 + s],
        )
        for s in range(4)
    ]

    pl.semaphore_wait(barrier, len(peers))
    sent = []

    def remote(src, dst, ssem, rsem, peer):
        c = pltpu.make_async_remote_copy(
            src_ref=src,
            dst_ref=dst,
            send_sem=ssem,
            recv_sem=rsem,
            device_id=peer,
            device_id_type=MESH,
        )
        c.start()
        sent.append(c)
        return c

    early = first_down + PIECES // 2

    def send_far(first, last):
        for k in range(first, last):
            source, place = chunks[k]
            far.append(remote(source, place(2), w_send.at[1, k], w_recv.at[1, k], across))

    far = []
    send_far(0, early)
    near = [remote(s, p(1), w_send.at[0, k], w_recv.at[0, k], mate) for k, (s, p) in enumerate(chunks)]

    values = tokens[...].astype(jnp.float32)
    scale = lax.rsqrt(jnp.mean(values * values, axis=-1, keepdims=True) + 1e-06)
    xb[0, 0] = (values * scale * gain[...]).astype(jnp.bfloat16)
    table = jnp.zeros(wtb.shape[2:], jnp.float32)
    rows_of = lax.broadcasted_iota(jnp.int32, wtb.shape[2:], 0)
    for k in range(ids.shape[0]):
        hit = (ids[k : k + 1, :] == rows_of) & (dropped[k : k + 1, :] == 0)
        table = table + jnp.where(hit, gates[k : k + 1, :], 0.0)
    wtb[0, 0] = table

    half = rows // 2
    parts = [(wtb, ())] + [(xb, (pl.ds(i * half, half),)) for i in range(2)]

    def part_of(i, side, r):
        ref, cut = parts[i]
        return ref.at[(side, r) + cut]

    rz, ry = [None], []
    for r in range(1, n_rows_z):
        rz.append(
            [
                remote(
                    part_of(i, 0, 0), part_of(i, 0, r), z_send.at[i, r], z_recv.at[i, r], along[r]
                )
                for i in range(3)
            ]
        )

    def to_side(r):
        ry.append([])
        for i in range(3):
            if r:
                rz[r][i].wait_recv()
            ry[r].append(
                remote(
                    part_of(i, 0, r), part_of(i, 1, r), y_send.at[i, r], y_recv.at[i, r], beside
                )
            )

    to_side(0)
    share_near = remote(xb.at[0, 0], sb.at[1], t_send.at[0], t_recv.at[0], mate)
    share_far = remote(xb.at[0, 0], sb.at[2], t_send.at[1], t_recv.at[1], across)
    send_far(early, n)

    passed = []

    def pass_on(k):
        far[k].wait_recv()
        place = chunks[k][1]
        passed.append(remote(place(2), place(3), w_send.at[2, k], w_recv.at[2, k], mate))

    def column(side, r, e):
        line = jnp.sum(
            jnp.where(rows_of == ep * experts + e, wtb[side, r], 0.0), axis=0, keepdims=True
        )
        return jnp.transpose(jnp.broadcast_to(line, (rows, rows)))[:, 0:1]

    def gate_only(first, count, e):
        def body(r, carry):
            left = jnp.concatenate([xb[0, r], xb[1, r]], axis=0)
            ga[r] = dot(left, gu[e, 0, 2:4].reshape(2 * hid, width), NT)
            return carry

        lax.fori_loop(first, first + count, body, 0)

    def hidden(first, count, pair, e_first, e_count, stored=False):
        def body(i, carry):
            e = e_first + i % e_count
            r = first + i // e_count
            left = jnp.concatenate([xb[0, r], xb[1, r]], axis=0)
            if stored:
                g = ga[r]
            else:
                g = dot(left, gu[e, 0, 2 * pair : 2 * pair + 2].reshape(2 * hid, width), NT)
            u = dot(left, gu[e, 1, 2 * pair : 2 * pair + 2].reshape(2 * hid, width), NT)
            weight = jnp.concatenate([column(0, r, e), column(1, r, e)], axis=0)
            h = (g * jax.nn.sigmoid(g) * u * weight).astype(jnp.bfloat16)
            hb[0, e, pair, r] = h[:rows]
            hb[1, e, pair, r] = h[rows:]
            return carry

        lax.fori_loop(0, count * e_count, body, 0)

    def shared_hidden(pair):
        left = xb[0, 0] if pair == 0 else sb[2]
        left = jnp.concatenate([left, sb[2 * pair + 1]], axis=0)
        g = dot(left, sg[...], NT)
        u = dot(left, su[...], NT)
        h = (g * jax.nn.sigmoid(g) * u).astype(jnp.bfloat16)
        sh[2 * pair] = h[:rows]
        sh[2 * pair + 1] = h[rows:]

    for k in range(first_down):
        own[k].wait()
        near[k].wait_recv()
    to_side(1)
    for c in ry[0]:
        c.wait_recv()
    hidden(0, 1, 0, 0, experts)
    for c in shared_in:
        c.wait()
    share_near.wait_recv()
    shared_hidden(0)
    shs = [remote(sh.at[1], whid.at[1], h_send.at[0], h_recv.at[0], mate)]
    pass_on(0)
    for c in ry[1]:
        c.wait_recv()
    hidden(1, 1, 0, 0, experts)
    to_side(2)
    pass_on(1)
    passed[0].wait_recv()
    passed[1].wait_recv()
    hidden(0, 2, 1, 0, 1)
    for c in ry[2]:
        c.wait_recv()
    hidden(2, 1, 0, 0, experts)
    hidden(2, 1, 1, 0, 1)
    to_side(3)
    pass_on(2)
    passed[2].wait_recv()
    gate_only(0, 3, 1)
    for c in ry[3]:
        c.wait_recv()
    hidden(3, 1, 0, 0, experts)
    hidden(3, 1, 1, 0, 1)
    gate_only(3, 1, 1)
    pass_on(3)
    passed[3].wait_recv()
    hidden(0, n_rows_z, 1, 1, 1, stored=True)

    ryd, rzd = [], []

    def down(c, side):
        cut = pl.ds(c * piece, piece)

        def body(q, carry):
            total = None
            for e in range(experts):
                for pair in range(2):
                    left = hb[side, e, pair, pl.ds(2 * q, 2)].reshape(2 * rows, 2 * hid)
                    right = db[e, 2 * pair : 2 * pair + 2, :, cut].reshape(2 * hid, piece)
                    part = dot(left, right, NN)
                    total = part if total is None else total + part
            total = total.reshape(2, rows, piece)
            if side:
                ysend[c, pl.ds(2 * q, 2)] = total.astype(jnp.bfloat16)
            else:
                ypart[c, pl.ds(2 * q, 2)] = total
            return carry

        lax.fori_loop(0, n_rows_z // 2, body, 0)

    def turn(c):
        ryd[c].wait_recv()
        for r in range(1, n_rows_z):
            both = ypart[c, r] + yrecv[c, r].astype(jnp.float32)
            zsend[c, r] = both.astype(jnp.bfloat16)
        rzd.append(
            [
                remote(zsend.at[c, r], zrecv.at[c, r], rz_send.at[c, r], rz_recv.at[c, r], along[r])
                for r in range(1, n_rows_z)
            ]
        )

    for c in range(PIECES):
        k = first_down + c
        own[k].wait()
        near[k].wait_recv()
        pass_on(k)
        passed[k].wait_recv()
        down(c, 1)
        ryd.append(remote(ysend.at[c], yrecv.at[c], ry_send.at[c], ry_recv.at[c], beside))
        down(c, 0)
        if c:
            turn(c - 1)
        if c == PIECES - 3:
            share_far.wait_recv()
            share_on = remote(sb.at[2], sb.at[3], t_send.at[2], t_recv.at[2], mate)
            share_on.wait_recv()
            shared_hidden(1)
            shs.append(remote(sh.at[2], whid.at[2], h_send.at[1], h_recv.at[1], across))
            shs.append(remote(sh.at[3], whid.at[3], h_send.at[2], h_recv.at[2], diagonal))

    for c in shared_down_in:
        c.wait()
    for c in shs:
        c.wait_recv()

    def base(c, carry):
        cut = pl.ds(pl.multiple_of(c * piece, piece), piece)
        total = tokens[:, cut].astype(jnp.float32) + dot(sh[0], sd[0, :, cut], NN)
        for s in range(1, 4):
            total = total + dot(whid[s], sd[s, :, cut], NN)
        ypart[c, 0] = ypart[c, 0] + total
        return carry

    lax.fori_loop(0, PIECES, base, 0)
    turn(PIECES - 1)
    for c in range(PIECES):
        cut = pl.ds(c * piece, piece)
        total = ypart[c, 0] + yrecv[c, 0].astype(jnp.float32)
        for r in range(1, n_rows_z):
            rzd[c][r - 1].wait_recv()
            total = total + zrecv[c, r].astype(jnp.float32)
        out[:, cut] = total.astype(out.dtype)
    for c in sent:
        c.wait_send()


def scratch_of(n_rows_z, rows, width, n_experts, experts, hid, shid):
    bf, f4 = jnp.bfloat16, jnp.float32
    piece = width // PIECES
    lines = n_experts
    pad = lambda v: -(-v // 128) * 128
    shapes = [
        ((COLS, n_rows_z, rows, width), bf),
        ((COLS, n_rows_z, lines, rows), f4),
        ((experts, 2, 4, hid, width), bf),
        ((n_rows_z, 2 * rows, 2 * hid), f4),
        ((experts, 4, hid, width), bf),
        ((COLS, experts, 2, n_rows_z, rows, 2 * hid), bf),
        ((4, rows, width), bf),
        ((shid, width), bf),
        ((shid, width), bf),
        ((4, shid, width), bf),
        ((4, rows, shid), bf),
        ((4, rows, shid), bf),
        ((PIECES, n_rows_z, rows, piece), bf),
        ((PIECES, n_rows_z, rows, piece), bf),
        ((PIECES, n_rows_z, rows, piece), f4),
        ((PIECES, n_rows_z, rows, piece), bf),
        ((PIECES, n_rows_z, rows, piece), bf),
    ]
    total = 0
    for dims, kind in shapes:
        size = pad(dims[-1]) * jnp.dtype(kind).itemsize
        for d in dims[:-1]:
            size *= d
        total += size
    n = 2 * experts + PIECES
    dma = pltpu.SemaphoreType.DMA
    sems = [dma((3, n)), dma((3, n)), dma((n + 6,))]
    sems += [dma((3, n_rows_z)) for _ in range(4)]
    sems += [dma((3,)) for _ in range(4)]
    sems += [dma((PIECES,)) for _ in range(2)]
    sems += [dma((PIECES, n_rows_z)) for _ in range(2)]
    return [pltpu.VMEM(d, k) for d, k in shapes] + sems, total


def fused(n_rows_z, scratch, tokens, gain, ids, slot, dropped, gates, wg, wu, wd, sg, su, sd):
    vmem = pl.BlockSpec(memory_space=pltpu.VMEM)
    hbm = pl.BlockSpec(memory_space=pl.ANY)
    return pl.pallas_call(
        functools.partial(layer_kernel, n_rows_z),
        out_shape=jax.ShapeDtypeStruct(tokens.shape, tokens.dtype),
        in_specs=[vmem] * 5 + [hbm] * 6,
        out_specs=vmem,
        scratch_shapes=scratch,
        compiler_params=pltpu.CompilerParams(
            collective_id=0, has_side_effects=True, vmem_limit_bytes=VMEM_BYTES
        ),
        name="moe_layer",
    )(
        tokens,
        gain[None, :],
        ids.T,
        dropped.T,
        gates.T,
        wg.transpose(0, 2, 1),
        wu.transpose(0, 2, 1),
        wd.transpose(0, 2, 1),
        sg.T,
        su.T,
        sd,
    )


TOP = 6
EXP_DEV = 2
TOK_DEV = 128


norm_eps = 1e-06


def swiglu(left, right):
    return jax.nn.silu(left) * right


def on_device(
    tokens,
    norm_gain,
    expert_ids,
    slot_index,
    dropped,
    gates,
    w_gate,
    w_up,
    w_down,
    shared_gate,
    shared_up,
    shared_down,
):
    n_expert_groups = lax.axis_size("ep")
    experts = EXP_DEV * n_expert_groups
    capacity = TOK_DEV * TOP * 4 // (experts * 3)
    model_width = tokens.shape[1]
    local_rows = tokens.shape[0]
    values = tokens.astype(jnp.float32)
    scale = lax.rsqrt(jnp.mean(values * values, axis=-1, keepdims=True) + norm_eps)
    normed = (values * scale * norm_gain).astype(jnp.bfloat16)
    destination_position = expert_ids * capacity + slot_index
    kept_pair = dropped == 0
    matrix_breadth = lax.iota(jnp.int32, experts * capacity)
    matches = (destination_position[:, :, None] == matrix_breadth[None, None, :]) & kept_pair[
        :, :, None
    ]
    dispatch_table = jnp.any(matches, axis=1).astype(jnp.bfloat16)
    outgoing = lax.dot_general(
        dispatch_table, normed, (((0,), (0,)), ((), ())), preferred_element_type=jnp.float32
    ).astype(jnp.bfloat16)
    boxes = outgoing.reshape(n_expert_groups, EXP_DEV, capacity, model_width)
    received = lax.all_to_all(boxes, "ep", split_axis=0, concat_axis=0, tiled=True)
    gate_all = lax.all_gather(w_gate, "tp", axis=2, tiled=True)
    up_all = lax.all_gather(w_up, "tp", axis=2, tiled=True)
    down_all = lax.all_gather(w_down, "tp", axis=2, tiled=True)
    gate_act = jnp.einsum("iecd,edf->iecf", received, gate_all, preferred_element_type=jnp.float32)
    up_act = jnp.einsum("iecd,edf->iecf", received, up_all, preferred_element_type=jnp.float32)
    hidden = swiglu(gate_act, up_act).astype(jnp.bfloat16)
    expert_out = jnp.einsum(
        "iecf,edf->iecd", hidden, down_all, preferred_element_type=jnp.float32
    ).astype(jnp.bfloat16)
    returned_output = lax.all_to_all(expert_out, "ep", split_axis=0, concat_axis=0, tiled=True)
    returned_rows = returned_output.reshape(experts * capacity, model_width)
    shard_piece = lax.all_gather(normed, "tp", axis=0, tiled=True)
    gate_act = jnp.dot(shard_piece, shared_gate, preferred_element_type=jnp.float32)
    up_act = jnp.dot(shard_piece, shared_up, preferred_element_type=jnp.float32)
    partial_hidden = swiglu(gate_act, up_act).astype(jnp.bfloat16)
    whole_hidden = lax.all_to_all(partial_hidden, "tp", split_axis=0, concat_axis=1, tiled=True)
    shared_out = jnp.dot(whole_hidden, shared_down, preferred_element_type=jnp.float32)
    safe_target = jnp.where(kept_pair, destination_position, 0)
    picked = jnp.take(returned_rows, safe_target.reshape(-1), axis=0).reshape(
        local_rows, TOP, model_width
    )
    kept_weights = jnp.where(kept_pair, gates, jnp.float32(0.0))
    routed = jnp.sum(picked.astype(jnp.float32) * kept_weights[:, :, None], axis=1)
    return (values + shared_out + routed).astype(jnp.bfloat16)


def solution(mesh):
    ep, tp = mesh.shape["ep"], mesh.shape["tp"]
    placed = (
        P(("ep", "tp"), None),
        P(),
        P(("ep", "tp"), None),
        P(("ep", "tp"), None),
        P(("ep", "tp"), None),
        P(("ep", "tp"), None),
        P("ep", None, "tp"),
        P("ep", None, "tp"),
        P("ep", None, "tp"),
        P(None, "tp"),
        P(None, "tp"),
        P(),
    )

    def layer(*args):
        tokens, w_gate, shared_gate = args[0], args[6], args[9]
        n_rows_z = ep // COLS
        scratch, size = scratch_of(
            n_rows_z,
            tokens.shape[0],
            tokens.shape[1],
            ep * w_gate.shape[0],
            w_gate.shape[0],
            w_gate.shape[2],
            shared_gate.shape[1],
        )
        spare = 8 * 1024 * 1024
        if tp == 2 * CORES and n_rows_z == 4 and w_gate.shape[0] == 2 and size + spare < VMEM_BYTES:
            return fused(n_rows_z, scratch, *args)
        return on_device(*args)

    return jax.shard_map(
        layer, mesh=mesh, in_specs=placed, out_specs=P(("ep", "tp"), None), check_vma=False
    )
```

profile of v0, /device:TPU:0, one launch (start us, length us, event | category | flops | bytes accessed | tf_op | source)
XLA Modules:
  0.0 140.3 jit_solution(35618323193011592)
XLA Ops:
  0.0 138.4 %moe_layer.1 = bf16[128,2048]{1,0:T(8,128)(2,1)} custom-call(bf16[128,2048]{1,0:T(8,128)(2,1)} %tokens.1, f32[1,2048]{1,0:T(1,128)} %bitcast.14, s32[6,128]{1,0:T(8,128)} %bitcast.15, s32[6,128]{1,0:T(8,128)} %bitcast.16, f32[6,128]{1,0:T(8,128)} %bitcast.17, bf16[2,176,2048]{2,1,0:T(8,128)(2,1)} %bitcast.9, bf16[2,176,2048]{2,1,0:T(8,128)(2,1)} %bitcast.10, ...), custom_call_target="tpu_custom_call" | custom-call | tf_op jit(solution)/shard_map/moe_layer/pallas_call | solution.py:408
  138.5 1.9 %copy.13 = bf16[128,2048]{1,0:T(8,128)(2,1)} copy(bf16[128,2048]{1,0:T(8,128)(2,1)} %moe_layer.1) | data formatting | bytes 1048576
where the time goes:
time: 141 us; the launch traced here: 140 us
  Pallas kernels  138 us (98%)
  local copies, waits for them, and re-layouts  1.88 us (1%)
    pallas_call x1, Pallas kernels, fused(): pl.pallas_call(functools.partial(layer_kernel, n_rows_z), out_shape=jax.S...  138 us

commit v1 on v0

v1 whole, which is shorter than its diff:
```python
import functools

import jax
import jax.numpy as jnp
from jax import lax
from jax.experimental import pallas as pl
from jax.experimental.pallas import tpu as pltpu
from jax.sharding import PartitionSpec as P

MESH = pl.DeviceIdType.MESH
CORES = 2
COLS = 2
VMEM_BYTES = 62 * 1024 * 1024
LANES = 128

NT = (((1,), (1,)), ((), ()))
NN = (((1,), (0,)), ((), ()))


def dot(a, b, dims):
    return lax.dot_general(a, b, dims, preferred_element_type=jnp.float32)


def flip(index, mask, size):
    out, bit = 0, 1
    while bit < size:
        digit = (index // bit) % 2
        out = out + (1 - digit if mask & bit else digit) * bit
        bit *= 2
    return out


def cuts_of(width):
    inside = width - 4 * LANES
    sizes = [LANES] * 2 + [2 * LANES] * (inside // (2 * LANES)) + [LANES] * 2
    starts = [sum(sizes[:i]) for i in range(len(sizes))]
    return [pl.ds(*cut) for cut in zip(starts, sizes)]


def layer_kernel(
    n_rows_z,
    tokens_in,
    gain_in,
    ids_in,
    dropped_in,
    gates_in,
    w_gate,
    w_up,
    w_down,
    s_gate,
    s_up,
    s_down,
    result,
    tokens,
    gain,
    ids,
    dropped,
    gates,
    out,
    xb,
    wtb,
    gu,
    ga0,
    ga1,
    db,
    hb,
    hl0,
    hl1,
    sb,
    sg,
    su,
    sd,
    sh,
    whid,
    ysend,
    yrecv,
    ypart,
    zsend,
    zrecv,
    own_sem,
    near_send,
    near_recv,
    far_send,
    far_recv,
    pass_send,
    pass_recv,
    z_send,
    z_recv,
    y_send,
    y_recv,
    t_send,
    t_recv,
    h_send,
    h_recv,
    ry_send,
    ry_recv,
    rz_send,
    rz_join,
    rz_recv,
    go,
    in_sem,
    out_sem,
):
    ep, tp = lax.axis_index("ep"), lax.axis_index("tp")
    z, y = ep // COLS, ep % COLS
    x, core = tp // CORES, tp % CORES
    rows, width = tokens.shape
    experts = w_gate.shape[0]
    hid = w_gate.shape[1]
    shid = s_gate.shape[0]
    cuts = cuts_of(width)
    pieces = len(cuts)
    split = hl0.shape[-1] // 2
    last = experts - 1
    mate = (ep, x * CORES + 1 - core)
    across = (ep, (1 - x) * CORES + core)
    diagonal = (ep, (1 - x) * CORES + 1 - core)
    beside = (z * COLS + 1 - y, tp)
    along = [None] + [(flip(z, r, n_rows_z) * COLS + y, tp) for r in range(1, n_rows_z)]
    at_end = jnp.where(z % 3 == 0, 1, 0)
    inner = at_end == 0
    order = [0, 1, 3 - at_end, 2 + at_end]

    barrier = pltpu.get_barrier_semaphore()
    peers = [mate, across, diagonal, beside] + along[1:]
    for peer in peers:
        pl.semaphore_signal(barrier, inc=1, device_id=peer, device_id_type=MESH)

    def local(src, dst, sem):
        c = pltpu.make_async_copy(src, dst, sem)
        c.start()
        return c

    inputs = [
        local(src, dst, in_sem.at[i])
        for i, (src, dst) in enumerate(
            (
                (tokens_in, tokens),
                (gain_in, gain),
                (ids_in, ids),
                (dropped_in, dropped),
                (gates_in, gates),
            )
        )
    ]
    chunks = []

    def add_chunk(source, e, m, start, size):
        rows_cut = pl.ds(start, size)
        chunks.append((source.at[e, rows_cut], lambda s: gu.at[e, m, s, rows_cut]))

    for e in range(experts):
        add_chunk(w_gate, e, 0, 0, hid)
        if e < last:
            add_chunk(w_up, e, 1, 0, hid)
        else:
            add_chunk(w_up, e, 1, 0, split)
            add_chunk(w_up, e, 1, split, hid - split)
    first_down = len(chunks)
    for cut in cuts:
        chunks.append(
            (w_down.at[:, :, cut], functools.partial(lambda cut, s: db.at[:, s, :, cut], cut))
        )
    n = len(chunks)

    def whole(s):
        return [(w_gate, gu.at[:, 0, s]), (w_up, gu.at[:, 1, s]), (w_down, db.at[:, s])]

    own = [local(src, dst, own_sem.at[i]) for i, (src, dst) in enumerate(whole(0))]
    shared_in = [local(s_gate, sg, own_sem.at[3]), local(s_up, su, own_sem.at[4])]
    who = [tp, mate[1], across[1], diagonal[1]]
    for s in range(4):
        local(
            s_down.at[pl.ds(pl.multiple_of(who[s] * shid, 16), shid), :],
            sd.at[pl.ds(s * shid, shid)],
            own_sem.at[5],
        )

    pl.semaphore_wait(barrier, len(peers))
    def copy_to(src, dst, ssem, rsem, peer):
        return pltpu.make_async_remote_copy(
            src_ref=src,
            dst_ref=dst,
            send_sem=ssem,
            recv_sem=rsem,
            device_id=peer,
            device_id_type=MESH,
        )

    def remote(src, dst, ssem, rsem, peer):
        c = copy_to(src, dst, ssem, rsem, peer)
        c.start()
        return c

    def group(k):
        return 0 if k < first_down else 1

    far = [
        copy_to(source, place(2), far_send.at[group(k)], far_recv.at[k], across)
        for k, (source, place) in enumerate(chunks)
    ]
    late = range(first_down + 1, n)
    for k in [*range(first_down - 1), first_down, first_down - 1]:
        far[k].start()

    @pl.when(core == 0)
    def _():
        for k in late:
            far[k].start()

    near = [
        remote(src, dst, near_send.at[i], near_recv.at[i], mate)
        for i, (src, dst) in enumerate(whole(1))
    ]

    for c in inputs:
        c.wait()
    values = tokens[...].astype(jnp.float32)
    scale = lax.rsqrt(jnp.mean(values * values, axis=-1, keepdims=True) + 1e-06)
    xb[0, 0] = (values * scale * gain[...]).astype(jnp.bfloat16)
    table = jnp.zeros(wtb.shape[2:], jnp.float32)
    rows_of = lax.broadcasted_iota(jnp.int32, wtb.shape[2:], 0)
    for k in range(ids.shape[0]):
        hit = (ids[k : k + 1, :] == rows_of) & (dropped[k : k + 1, :] == 0)
        table = table + jnp.where(hit, gates[k : k + 1, :], 0.0)
    wtb[0, 0] = table

    half = rows // 2
    parts = 3

    def part(i, side, slot):
        if i == 0:
            return wtb.at[side, slot]
        return xb.at[side, slot, pl.ds((i - 1) * half, half)]

    routes = [(0, 1, 1), (0, 3, 3), (1, 2, 3), (3, 2, 1), (2, 3, 1)]
    hops = [
        [
            copy_to(
                part(i, 0, src),
                part(i, 0, dst),
                z_send.at[min(k, 1), min(i, 1)],
                z_recv.at[i, dst - 1],
                along[by],
            )
            for i in range(parts)
        ]
        for k, (src, dst, by) in enumerate(routes)
    ]

    def arrived(i, slot):
        copy_to(
            part(i, 0, 0), part(i, 0, slot), z_send.at[0, 0], z_recv.at[i, slot - 1], along[1]
        ).wait_recv()

    def to_side(k, i):
        slot = order[k]
        m = min(i, 1)
        remote(part(i, 0, slot), part(i, 1, slot), y_send.at[m], y_recv.at[m, k], beside)

    def from_side(k):
        for m, ref in enumerate((wtb, xb)):
            slot = ref.at[1, order[k]]
            copy_to(slot, slot, y_send.at[m], y_recv.at[m, k], beside).wait_recv()

    for i in range(parts):
        hops[0][i].start()

    @pl.when(inner)
    def _():
        for i in range(parts):
            hops[1][i].start()

    for i in range(parts):
        to_side(0, i)
    share_near = remote(xb.at[0, 0], sb.at[1], t_send, t_recv.at[0], mate)
    share_far = copy_to(xb.at[0, 0], sb.at[2], t_send, t_recv.at[1], across)

    @pl.when(core == 0)
    def _():
        share_far.start()

    passed = {}

    def pass_on(k):
        far[k].wait_recv()
        place = chunks[k][1]
        passed[k] = remote(place(2), place(3), pass_send.at[group(k)], pass_recv.at[k], mate)

    def column(side, r, e):
        line = jnp.sum(
            jnp.where(rows_of == ep * experts + e, wtb[side, r], 0.0), axis=0, keepdims=True
        )
        return jnp.transpose(jnp.broadcast_to(line, (rows, rows)))[:, 0:1]

    def both_sides(r):
        return jnp.concatenate([xb[0, r], xb[1, r]], axis=0)

    def two_rows(side, q):
        return xb[side, pl.ds(2 * q, 2)].reshape(2 * rows, width)

    def matrix(e, m, pair, start, size):
        picked = gu[e, m, 2 * pair : 2 * pair + 2, start : start + size]
        return picked.reshape(2 * size, width)

    def activate(g, u, r, e):
        weight = jnp.concatenate([column(0, r, e), column(1, r, e)], axis=0)
        return (g * jax.nn.sigmoid(g) * u * weight).astype(jnp.bfloat16)

    def hidden(r, pair, e):
        left = both_sides(r)
        g = dot(left, matrix(e, 0, pair, 0, hid), NT)
        u = dot(left, matrix(e, 1, pair, 0, hid), NT)
        h = activate(g, u, r, e)
        hb[0, e * 2 + pair, r] = h[:rows]
        hb[1, e * 2 + pair, r] = h[rows:]

    def near_hidden(k):
        def body(e, carry):
            hidden(order[k], 0, e)
            return carry

        lax.fori_loop(0, experts, body, 0)

    def far_hidden(first, count):
        def body(i, carry):
            r = i
            for k in range(1, n_rows_z):
                r = jnp.where(i == k, order[k], r)
            hidden(r, 1, 0)
            return carry

        lax.fori_loop(first, first + count, body, 0)

    def last_gate():
        def body(i, carry):
            left = two_rows(i // 2, i % 2)
            ga0[i] = dot(left, matrix(last, 0, 1, 0, split), NT)
            ga1[i] = dot(left, matrix(last, 0, 1, split, hid - split), NT)
            return carry

        lax.fori_loop(0, n_rows_z, body, 0)

    def last_up(stored, start, size, place, side):
        def body(q, carry):
            u = dot(two_rows(side, q), matrix(last, 1, 1, start, size), NT)
            g = stored[2 * side + q]
            weight = [column(side, 2 * q + i, last) for i in range(2)]
            h = g * jax.nn.sigmoid(g) * u * jnp.concatenate(weight, axis=0)
            place[side, pl.ds(2 * q, 2)] = h.astype(jnp.bfloat16).reshape(2, rows, 2 * size)
            return carry

        lax.fori_loop(0, n_rows_z // 2, body, 0)

    def shared_hidden(pair):
        left = xb[0, 0] if pair == 0 else sb[2]
        left = jnp.concatenate([left, sb[2 * pair + 1]], axis=0)
        g = dot(left, sg[...], NT)
        u = dot(left, su[...], NT)
        h = (g * jax.nn.sigmoid(g) * u).astype(jnp.bfloat16)
        sh[2 * pair] = h[:rows]
        sh[2 * pair + 1] = h[rows:]

    for i in range(2):
        own[i].wait()
        near[i].wait_recv()
    for i in range(parts):
        arrived(i, 1)
        to_side(1, i)

        @pl.when(inner)
        def _(i=i):
            hops[2][i].start()
            arrived(i, 3)
            hops[3][i].start()

    from_side(0)
    near_hidden(0)
    for c in shared_in:
        c.wait()
    share_near.wait_recv()
    shared_hidden(0)
    share_back = remote(sh.at[1], whid.at[1], h_send, h_recv.at[0], mate)
    pass_on(0)
    for i in range(parts):

        @pl.when(inner)
        def _(i=i):
            arrived(i, 2)
            hops[4][i].start()

        @pl.when(at_end == 1)
        def _(i=i):
            arrived(i, 2)

        to_side(2, i)
    from_side(1)
    near_hidden(1)
    for i in range(parts):

        @pl.when(at_end == 1)
        def _(i=i):
            arrived(i, 3)

        to_side(3, i)
        if i == 1:
            pass_on(1)
            passed[0].wait_recv()
            passed[1].wait_recv()
            far_hidden(0, 2)
    from_side(2)
    near_hidden(2)
    far_hidden(2, 1)
    from_side(3)
    near_hidden(3)
    far_hidden(3, 1)
    pass_on(2)
    passed[2].wait_recv()
    last_gate()
    pass_on(3)
    passed[3].wait_recv()
    for side in range(COLS):
        last_up(ga0, 0, split, hl0, side)
    pass_on(first_down)
    pass_on(first_down - 1)

    @pl.when(core == 0)
    def _():
        pl.semaphore_signal(go, inc=1, device_id=mate, device_id_type=MESH)

    @pl.when(core == 1)
    def _():
        pl.semaphore_wait(go, 1)
        for k in late:
            far[k].start()
        share_far.start()

    passed[first_down - 1].wait_recv()
    last_up(ga1, split, hid - split, hl1, 1)

    def down(c, side):
        cut = cuts[c]
        piece = cut.size

        def body(q, carry):
            total = None

            def add(total, left, e, pair, start, size):
                left = left.reshape(2 * rows, 2 * size)
                right = db[e, 2 * pair : 2 * pair + 2, start : start + size, cut]
                part = dot(left, right.reshape(2 * size, piece), NN)
                return part if total is None else total + part

            two = pl.ds(2 * q, 2)
            for e in range(experts):
                for pair in range(2):
                    if 2 * e + pair < 2 * experts - 1:
                        total = add(total, hb[side, 2 * e + pair, two], e, pair, 0, hid)
            total = add(total, hl0[side, two], last, 1, 0, split)
            total = add(total, hl1[side, two], last, 1, split, hid - split)
            total = total.reshape(2, rows, piece)
            if side:
                ysend[two, :, cut] = total.astype(jnp.bfloat16)
            else:
                ypart[two, :, cut] = total
            return carry

        lax.fori_loop(0, n_rows_z // 2, body, 0)

    end = pieces - 1

    def side_leg(c, r):
        sem = ry_recv.at[c + (n_rows_z - 1 - r if c == end else 0)]
        span = r if c == end else pl.ds(0, n_rows_z)
        return copy_to(
            ysend.at[span, :, cuts[c]], yrecv.at[span, :, cuts[c]], ry_send, sem, beside
        )

    def send_side(c):
        for r in range(n_rows_z - 1, -1, -1) if c == end else (0,):
            side_leg(c, r).start()

    def block(c, r, extra=None):
        cut = cuts[c]
        total = ypart[r, :, cut] + yrecv[r, :, cut].astype(jnp.float32)
        if extra is not None:
            total = total + zrecv[extra, :, cut].astype(jnp.float32)
        zsend[r, :, cut] = total.astype(jnp.bfloat16)

    def leg(c, r, slot, by, sem):
        return copy_to(
            zsend.at[r, :, cuts[c]], zrecv.at[slot, :, cuts[c]], rz_send, sem, along[by]
        )

    def join_sem(c, slot):
        return rz_join.at[c + (1 if c == end and slot == 2 else 0)]

    def last_sem(c):
        return rz_recv.at[max(c - end + 2, 0)]

    def turn(c):
        if c < end:
            side_leg(c, 0).wait_recv()

        @pl.when(at_end == 1)
        def _():
            for r, slot in ((3, 0), (2, 2), (1, 1)):
                if c == end:
                    side_leg(c, r).wait_recv()
                block(c, r)
                leg(c, r, slot, 1, join_sem(c, slot) if r > 1 else last_sem(c)).start()

        @pl.when(inner)
        def _():
            if c == end:
                for r in (3, 2, 1):
                    side_leg(c, r).wait_recv()
            block(c, 1)
            leg(c, 1, 1, 1, last_sem(c)).start()

        if c == end:
            side_leg(c, 0).wait_recv()

    def join(c):
        @pl.when(inner)
        def _():
            if c < end:
                both = zrecv.at[pl.ds(0, 2), :, cuts[c]]
                copy_to(both, both, rz_send, join_sem(c, 0), along[1]).wait_recv()
            for r, slot in ((2, 0), (3, 2)):
                if c == end:
                    leg(c, 1, slot, 1, join_sem(c, slot)).wait_recv()
                block(c, r, slot)
                leg(c, r, r, r, last_sem(c)).start()

    def base(first, stop, c):
        cut = cuts[c]
        total = ypart[0, :, cut]
        if first == 0:
            total = total + tokens[:, cut].astype(jnp.float32)
        for s in range(first, stop):
            left = sh[0] if s == 0 else whid[s]
            total = total + dot(left, sd[s * shid : (s + 1) * shid, cut], NN)
        ypart[0, :, cut] = total

    def landed(first, stop):
        start = cuts[first].start
        span = pl.ds(start, cuts[stop - 1].start + cuts[stop - 1].size - start)
        both = zrecv.at[pl.ds(0, 2), :, span]
        copy_to(both, both, rz_send, last_sem(first), along[1]).wait_recv()

    def final(c):
        cut = cuts[c]
        total = ypart[0, :, cut] + yrecv[0, :, cut].astype(jnp.float32)
        for slot in (1, order[2]):
            total = total + zrecv[slot, :, cut].astype(jnp.float32)
        out[:, cut] = total.astype(out.dtype)
        local(out.at[:, cut], result.at[:, cut], out_sem)

    own[2].wait()
    near[2].wait_recv()
    for c in range(pieces):
        k = first_down + c
        if k not in passed:
            pass_on(k)
        passed[k].wait_recv()
        down(c, 1)
        send_side(c)
        if c == 0:
            last_up(ga1, split, hid - split, hl1, 0)
        down(c, 0)
        if c == 0:
            pltpu.make_async_copy(s_down, sd, own_sem.at[5]).wait()
            share_back.wait_recv()
        base(0, 2, c)
        if c == end:
            share_far.wait_recv()
            share_on = remote(sb.at[2], sb.at[3], t_send, t_recv.at[2], mate)
        if 2 < c < end:
            pass_on(k + 1)
        if c > 2:
            join(c - 3)
        if c > 1:
            turn(c - 2)

    share_on.wait_recv()
    shared_hidden(1)
    remote(sh.at[2], whid.at[2], h_send, h_recv.at[1], across)
    remote(sh.at[3], whid.at[3], h_send, h_recv.at[1], diagonal)
    turn(end - 1)
    join(end - 2)
    turn(end)
    join(end - 1)
    join(end)
    both_back = whid.at[pl.ds(2, 2)]
    copy_to(both_back, both_back, h_send, h_recv.at[1], across).wait_recv()
    for c in range(pieces):
        base(2, 4, c)
    landed(0, end - 1)
    for c in range(end - 1):
        final(c)
    for c in (end - 1, end):
        landed(c, c + 1)
        final(c)

    def drain(ref, sem):
        copy_to(ref, ref, sem, near_recv.at[0], mate).wait_send()

    for c in near:
        c.wait_send()
    for sems in (far_send, pass_send):
        drain(gu.at[:, :, 2], sems.at[0])
        drain(db.at[:, 2], sems.at[1])
    for m, ref in enumerate((wtb, xb)):
        drain(ref.at[0, 0], z_send.at[0, m])
        drain(ref.at[0], y_send.at[m])
    drain(sb.at[pl.ds(0, 3)], t_send)
    drain(sh.at[pl.ds(0, 3)], h_send)
    drain(ysend, ry_send)
    drain(zsend.at[pl.ds(1, 3)], rz_send)

    @pl.when(inner)
    def _():
        for m, ref in enumerate((wtb, xb)):
            drain(ref.at[0], z_send.at[1, m])

    pltpu.make_async_copy(out, result, out_sem).wait()


def scratch_of(n_rows_z, rows, top, width, n_experts, experts, hid, shid):
    bf, f4 = jnp.bfloat16, jnp.float32
    pieces = len(cuts_of(width))
    lines = n_experts
    split = hid - hid // 32 * 16
    pad = lambda v: -(-v // 128) * 128
    shapes = [
        ((rows, width), bf),
        ((1, width), f4),
        ((top, rows), jnp.int32),
        ((top, rows), jnp.int32),
        ((top, rows), f4),
        ((rows, width), bf),
        ((COLS, n_rows_z, rows, width), bf),
        ((COLS, n_rows_z, lines, rows), f4),
        ((experts, 2, 4, hid, width), bf),
        ((n_rows_z, 2 * rows, 2 * split), f4),
        ((n_rows_z, 2 * rows, 2 * (hid - split)), f4),
        ((experts, 4, hid, width), bf),
        ((COLS, 2 * experts - 1, n_rows_z, rows, 2 * hid), bf),
        ((COLS, n_rows_z, rows, 2 * split), bf),
        ((COLS, n_rows_z, rows, 2 * (hid - split)), bf),
        ((4, rows, width), bf),
        ((shid, width), bf),
        ((shid, width), bf),
        ((4 * shid, width), bf),
        ((4, rows, shid), bf),
        ((4, rows, shid), bf),
        ((n_rows_z, rows, width), bf),
        ((n_rows_z, rows, width), bf),
        ((n_rows_z, rows, width), f4),
        ((n_rows_z, rows, width), bf),
        ((n_rows_z, rows, width), bf),
    ]
    total = 0
    for dims, kind in shapes:
        size = pad(dims[-1]) * jnp.dtype(kind).itemsize
        for d in dims[:-1]:
            size *= d
        total += size
    n = 2 * experts + 1 + pieces
    dma = pltpu.SemaphoreType.DMA
    one = pltpu.SemaphoreType.DMA
    sems = [dma((6,)), dma((3,)), dma((3,)), dma((2,)), dma((n,)), dma((2,)), dma((n,))]
    sems += [dma((2, 2)), dma((3, n_rows_z - 1)), dma((2,)), dma((2, n_rows_z))]
    sems += [one, dma((3,)), one, dma((2,))]
    sems += [one, dma((pieces + n_rows_z - 1,)), one, dma((pieces + 1,)), dma((3,))]
    sems += [pltpu.SemaphoreType.REGULAR, dma((5,)), one]
    return [pltpu.VMEM(d, k) for d, k in shapes] + sems, total


def fused(n_rows_z, scratch, tokens, gain, ids, slot, dropped, gates, wg, wu, wd, sg, su, sd):
    hbm = pl.BlockSpec(memory_space=pl.ANY)
    return pl.pallas_call(
        functools.partial(layer_kernel, n_rows_z),
        out_shape=jax.ShapeDtypeStruct(tokens.shape, tokens.dtype),
        in_specs=[hbm] * 11,
        out_specs=hbm,
        scratch_shapes=scratch,
        compiler_params=pltpu.CompilerParams(
            collective_id=0, has_side_effects=True, vmem_limit_bytes=VMEM_BYTES
        ),
        name="moe_layer",
    )(
        tokens,
        gain[None, :],
        ids.T,
        dropped.T,
        gates.T,
        wg.transpose(0, 2, 1),
        wu.transpose(0, 2, 1),
        wd.transpose(0, 2, 1),
        sg.T,
        su.T,
        sd,
    )


TOP = 6
EXP_DEV = 2
TOK_DEV = 128


norm_eps = 1e-06


def swiglu(left, right):
    return jax.nn.silu(left) * right


def on_device(
    tokens,
    norm_gain,
    expert_ids,
    slot_index,
    dropped,
    gates,
    w_gate,
    w_up,
    w_down,
    shared_gate,
    shared_up,
    shared_down,
):
    n_expert_groups = lax.axis_size("ep")
    experts = EXP_DEV * n_expert_groups
    capacity = TOK_DEV * TOP * 4 // (experts * 3)
    model_width = tokens.shape[1]
    local_rows = tokens.shape[0]
    values = tokens.astype(jnp.float32)
    scale = lax.rsqrt(jnp.mean(values * values, axis=-1, keepdims=True) + norm_eps)
    normed = (values * scale * norm_gain).astype(jnp.bfloat16)
    destination_position = expert_ids * capacity + slot_index
    kept_pair = dropped == 0
    matrix_breadth = lax.iota(jnp.int32, experts * capacity)
    matches = (destination_position[:, :, None] == matrix_breadth[None, None, :]) & kept_pair[
        :, :, None
    ]
    dispatch_table = jnp.any(matches, axis=1).astype(jnp.bfloat16)
    outgoing = lax.dot_general(
        dispatch_table, normed, (((0,), (0,)), ((), ())), preferred_element_type=jnp.float32
    ).astype(jnp.bfloat16)
    boxes = outgoing.reshape(n_expert_groups, EXP_DEV, capacity, model_width)
    received = lax.all_to_all(boxes, "ep", split_axis=0, concat_axis=0, tiled=True)
    gate_all = lax.all_gather(w_gate, "tp", axis=2, tiled=True)
    up_all = lax.all_gather(w_up, "tp", axis=2, tiled=True)
    down_all = lax.all_gather(w_down, "tp", axis=2, tiled=True)
    gate_act = jnp.einsum("iecd,edf->iecf", received, gate_all, preferred_element_type=jnp.float32)
    up_act = jnp.einsum("iecd,edf->iecf", received, up_all, preferred_element_type=jnp.float32)
    hidden = swiglu(gate_act, up_act).astype(jnp.bfloat16)
    expert_out = jnp.einsum(
        "iecf,edf->iecd", hidden, down_all, preferred_element_type=jnp.float32
    ).astype(jnp.bfloat16)
    returned_output = lax.all_to_all(expert_out, "ep", split_axis=0, concat_axis=0, tiled=True)
    returned_rows = returned_output.reshape(experts * capacity, model_width)
    shard_piece = lax.all_gather(normed, "tp", axis=0, tiled=True)
    gate_act = jnp.dot(shard_piece, shared_gate, preferred_element_type=jnp.float32)
    up_act = jnp.dot(shard_piece, shared_up, preferred_element_type=jnp.float32)
    partial_hidden = swiglu(gate_act, up_act).astype(jnp.bfloat16)
    whole_hidden = lax.all_to_all(partial_hidden, "tp", split_axis=0, concat_axis=1, tiled=True)
    shared_out = jnp.dot(whole_hidden, shared_down, preferred_element_type=jnp.float32)
    safe_target = jnp.where(kept_pair, destination_position, 0)
    picked = jnp.take(returned_rows, safe_target.reshape(-1), axis=0).reshape(
        local_rows, TOP, model_width
    )
    kept_weights = jnp.where(kept_pair, gates, jnp.float32(0.0))
    routed = jnp.sum(picked.astype(jnp.float32) * kept_weights[:, :, None], axis=1)
    return (values + shared_out + routed).astype(jnp.bfloat16)


def solution(mesh):
    ep, tp = mesh.shape["ep"], mesh.shape["tp"]
    placed = (
        P(("ep", "tp"), None),
        P(),
        P(("ep", "tp"), None),
        P(("ep", "tp"), None),
        P(("ep", "tp"), None),
        P(("ep", "tp"), None),
        P("ep", None, "tp"),
        P("ep", None, "tp"),
        P("ep", None, "tp"),
        P(None, "tp"),
        P(None, "tp"),
        P(),
    )

    def layer(*args):
        tokens, w_gate, shared_gate = args[0], args[6], args[9]
        n_rows_z = ep // COLS
        scratch, size = scratch_of(
            n_rows_z,
            tokens.shape[0],
            args[2].shape[1],
            tokens.shape[1],
            ep * w_gate.shape[0],
            w_gate.shape[0],
            w_gate.shape[2],
            shared_gate.shape[1],
        )
        spare = 8 * 1024 * 1024
        if tp == 2 * CORES and n_rows_z == 4 and w_gate.shape[0] == 2 and size + spare < VMEM_BYTES:
            return fused(n_rows_z, scratch, *args)
        return on_device(*args)

    return jax.shard_map(
        layer, mesh=mesh, in_specs=placed, out_specs=P(("ep", "tp"), None), check_vma=False
    )
```

time: 141 us -> 132 us (0.936)
  Pallas kernels: 138 us -> 130 us
    pallas_call x1, Pallas kernels: 138 us -> 130 us  [fused(): pl.pallas_call(functools.partial(layer_kernel, n_rows_z), out_shape=jax.S...]
where the time goes in v1:
time: 132 us
  Pallas kernels  130 us (98%)
  local copies, waits for them, and re-layouts  1.88 us (1%)
    pallas_call x1, Pallas kernels, fused(): pl.pallas_call(functools.partial(layer_kernel, n_rows_z), out_shape=jax.S...  130 us

profile of v1, /device:TPU:0, one launch (start us, length us, event | category | flops | bytes accessed | tf_op | source)
XLA Modules:
  0.0 132.2 jit_solution(12596805862350726111)
XLA Ops:
  0.0 130.3 %moe_layer.1 = bf16[128,2048]{1,0:T(8,128)(2,1)} custom-call(bf16[128,2048]{1,0:T(8,128)(2,1)} %tokens_in.1, f32[1,2048]{1,0:T(1,128)} %bitcast.14, s32[6,128]{1,0:T(8,128)} %bitcast.15, s32[6,128]{1,0:T(8,128)} %bitcast.16, f32[6,128]{1,0:T(8,128)} %bitcast.17, bf16[2,176,2048]{2,1,0:T(8,128)(2,1)} %bitcast.9, bf16[2,176,2048]{2,1,0:T(8,128)(2,1)} %bitcast.10, ...), custom_call_target="tpu_custom_call" | custom-call | tf_op jit(solution)/shard_map/moe_layer/pallas_call | solution.py:683
  130.4 1.9 %copy.13 = bf16[128,2048]{1,0:T(8,128)(2,1)} copy(bf16[128,2048]{1,0:T(8,128)(2,1)} %moe_layer.1) | data formatting | bytes 1048576

commit v2 on v1

--- a/solution.py
+++ b/solution.py
@@ -12,6 +12,7 @@
 COLS = 2
 VMEM_BYTES = 62 * 1024 * 1024
 LANES = 128
+SWING = 3
 
 NT = (((1,), (1,)), ((), ()))
 NN = (((1,), (0,)), ((), ()))
@@ -31,8 +32,8 @@
 
 
 def cuts_of(width):
-    inside = width - 4 * LANES
-    sizes = [LANES] * 2 + [2 * LANES] * (inside // (2 * LANES)) + [LANES] * 2
+    inside = width - 6 * LANES
+    sizes = [LANES] * 2 + [2 * LANES] * (inside // (2 * LANES)) + [LANES] * 4
     starts = [sum(sizes[:i]) for i in range(len(sizes))]
     return [pl.ds(*cut) for cut in zip(starts, sizes)]
 
@@ -77,6 +78,8 @@
     ypart,
     zsend,
     zrecv,
+    zsend2,
+    zrecv2,
     own_sem,
     near_send,
     near_recv,
@@ -97,6 +100,9 @@
     rz_send,
     rz_join,
     rz_recv,
+    sw_send,
+    sw_join,
+    sw_recv,
     go,
     in_sem,
     out_sem,
@@ -199,8 +205,8 @@
         copy_to(source, place(2), far_send.at[group(k)], far_recv.at[k], across)
         for k, (source, place) in enumerate(chunks)
     ]
-    late = range(first_down + 1, n)
-    for k in [*range(first_down - 1), first_down, first_down - 1]:
+    late = range(first_down + 2, n)
+    for k in [*range(first_down - 1), first_down, first_down - 1, first_down + 1]:
         far[k].start()
 
     @pl.when(core == 0)
@@ -352,14 +358,15 @@
 
         lax.fori_loop(0, n_rows_z // 2, body, 0)
 
-    def shared_hidden(pair):
-        left = xb[0, 0] if pair == 0 else sb[2]
-        left = jnp.concatenate([left, sb[2 * pair + 1]], axis=0)
+    def shared_act(left):
         g = dot(left, sg[...], NT)
         u = dot(left, su[...], NT)
-        h = (g * jax.nn.sigmoid(g) * u).astype(jnp.bfloat16)
-        sh[2 * pair] = h[:rows]
-        sh[2 * pair + 1] = h[rows:]
+        return (g * jax.nn.sigmoid(g) * u).astype(jnp.bfloat16)
+
+    def shared_hidden():
+        h = shared_act(jnp.concatenate([xb[0, 0], sb[1]], axis=0))
+        sh[0] = h[:rows]
+        sh[1] = h[rows:]
 
     for i in range(2):
         own[i].wait()
@@ -379,7 +386,7 @@
     for c in shared_in:
         c.wait()
     share_near.wait_recv()
-    shared_hidden(0)
+    shared_hidden()
     share_back = remote(sh.at[1], whid.at[1], h_send, h_recv.at[0], mate)
     pass_on(0)
     for i in range(parts):
@@ -533,6 +540,54 @@
                 block(c, r, slot)
                 leg(c, r, r, r, last_sem(c)).start()
 
+    def swing_leg(src, slot, by, sem):
+        return copy_to(src, zrecv2.at[slot], sw_send, sem, along[by])
+
+    swing = cuts[SWING]
+
+    def swing_out():
+        def ahead(r, slot, sem, sem2):
+            zsend[r, :, swing] = ypart[r, :, swing].astype(jnp.bfloat16)
+            leg(SWING, r, slot, 1, sem).start()
+            swing_leg(ysend.at[r, :, swing], slot, 1, sem2).start()
+
+        @pl.when(at_end == 1)
+        def _():
+            for r, slot in ((3, 0), (2, 2)):
+                ahead(r, slot, join_sem(SWING, slot), sw_join)
+            ahead(1, 1, last_sem(SWING), sw_recv)
+
+        @pl.when(inner)
+        def _():
+            ahead(1, 1, last_sem(SWING), sw_recv)
+
+    def swing_join():
+        @pl.when(inner)
+        def _():
+            both = zrecv.at[pl.ds(0, 2), :, swing]
+            copy_to(both, both, rz_send, join_sem(SWING, 0), along[1]).wait_recv()
+            both = zrecv2.at[pl.ds(0, 2)]
+            copy_to(both, both, sw_send, sw_join, along[1]).wait_recv()
+            for r, slot in ((2, 0), (3, 2)):
+                total = ypart[r, :, swing] + zrecv[slot, :, swing].astype(jnp.float32)
+                zsend[r, :, swing] = total.astype(jnp.bfloat16)
+                leg(SWING, r, r, r, last_sem(SWING)).start()
+                total = ysend[r, :, swing].astype(jnp.float32) + zrecv2[slot].astype(jnp.float32)
+                zsend2[r] = total.astype(jnp.bfloat16)
+                swing_leg(zsend2.at[r], r, r, sw_recv).start()
+
+    def swing_side():
+        return copy_to(zsend2.at[0], yrecv.at[0, :, swing], sw_send, ry_recv.at[SWING], beside)
+
+    def swing_cross():
+        both = zrecv2.at[pl.ds(0, 2)]
+        copy_to(both, both, sw_send, sw_recv, along[1]).wait_recv()
+        total = ysend[0, :, swing].astype(jnp.float32)
+        for slot in (1, order[2]):
+            total = total + zrecv2[slot].astype(jnp.float32)
+        zsend2[0] = total.astype(jnp.bfloat16)
+        swing_side().start()
+
     def base(first, stop, c):
         cut = cuts[c]
         total = ypart[0, :, cut]
@@ -557,6 +612,17 @@
         out[:, cut] = total.astype(out.dtype)
         local(out.at[:, cut], result.at[:, cut], out_sem)
 
+    steps = {
+        2: [lambda: turn(0)],
+        3: [swing_out, lambda: turn(1)],
+        4: [lambda: turn(2), lambda: join(0)],
+        6: [lambda: turn(4)],
+        7: [swing_join],
+        8: [lambda: join(1), lambda: turn(5)],
+        end: [lambda: join(2), lambda: turn(6), swing_cross],
+    }
+    rest = [lambda: turn(7), lambda: join(4), lambda: turn(8), lambda: join(5)]
+    steps[end] += rest
     own[2].wait()
     near[2].wait_recv()
     for c in range(pieces):
@@ -565,33 +631,35 @@
             pass_on(k)
         passed[k].wait_recv()
         down(c, 1)
-        send_side(c)
+        if c != SWING:
+            send_side(c)
         if c == 0:
+            pass_on(k + 1)
             last_up(ga1, split, hid - split, hl1, 0)
         down(c, 0)
         if c == 0:
             pltpu.make_async_copy(s_down, sd, own_sem.at[5]).wait()
             share_back.wait_recv()
         base(0, 2, c)
-        if c == end:
-            share_far.wait_recv()
-            share_on = remote(sb.at[2], sb.at[3], t_send, t_recv.at[2], mate)
-        if 2 < c < end:
+        if 0 < c < end:
             pass_on(k + 1)
-        if c > 2:
-            join(c - 3)
-        if c > 1:
-            turn(c - 2)
-
+        for step in steps.get(c, []):
+            step()
+
+    share_far.wait_recv()
+    share_on = remote(sb.at[2], sb.at[3], t_send, t_recv.at[2], mate)
+    sh[2] = shared_act(sb[2])
+    remote(sh.at[2], whid.at[2], h_send, h_recv.at[1], across)
     share_on.wait_recv()
-    shared_hidden(1)
-    remote(sh.at[2], whid.at[2], h_send, h_recv.at[1], across)
+    sh[3] = shared_act(sb[3])
     remote(sh.at[3], whid.at[3], h_send, h_recv.at[1], diagonal)
+    join(6)
     turn(end - 1)
-    join(end - 2)
+    join(7)
     turn(end)
-    join(end - 1)
-    join(end)
+    for c in range(end - 2, end + 1):
+        join(c)
+    swing_side().wait_recv()
     both_back = whid.at[pl.ds(2, 2)]
     copy_to(both_back, both_back, h_send, h_recv.at[1], across).wait_recv()
     for c in range(pieces):
@@ -616,7 +684,8 @@
         drain(ref.at[0], y_send.at[m])
     drain(sb.at[pl.ds(0, 3)], t_send)
     drain(sh.at[pl.ds(0, 3)], h_send)
-    drain(ysend, ry_send)
+    drain(ysend.at[:, :, pl.ds(0, width - swing.size)], ry_send)
+    drain(zsend2, sw_send)
     drain(zsend.at[pl.ds(1, 3)], rz_send)
 
     @pl.when(inner)
@@ -660,6 +729,8 @@
         ((n_rows_z, rows, width), f4),
         ((n_rows_z, rows, width), bf),
         ((n_rows_z, rows, width), bf),
+        ((n_rows_z, rows, 2 * LANES), bf),
+        ((n_rows_z, rows, 2 * LANES), bf),
     ]
     total = 0
     for dims, kind in shapes:
@@ -674,7 +745,7 @@
     sems += [dma((2, 2)), dma((3, n_rows_z - 1)), dma((2,)), dma((2, n_rows_z))]
     sems += [one, dma((3,)), one, dma((2,))]
     sems += [one, dma((pieces + n_rows_z - 1,)), one, dma((pieces + 1,)), dma((3,))]
-    sems += [pltpu.SemaphoreType.REGULAR, dma((5,)), one]
+    sems += [one] * 3 + [pltpu.SemaphoreType.REGULAR, dma((5,)), one]
     return [pltpu.VMEM(d, k) for d, k in shapes] + sems, total
 
 

time: 132 us -> 129 us (0.977)
  Pallas kernels: 130 us -> 127 us
    pallas_call x1, Pallas kernels: 130 us -> 127 us  [fused(): pl.pallas_call(functools.partial(layer_kernel, n_rows_z), out_shape=jax.S...]
where the time goes in v2:
time: 129 us
  Pallas kernels  127 us (98%)
  local copies, waits for them, and re-layouts  1.88 us (1%)
    pallas_call x1, Pallas kernels, fused(): pl.pallas_call(functools.partial(layer_kernel, n_rows_z), out_shape=jax.S...  127 us

profile of v2, /device:TPU:0, one launch (start us, length us, event | category | flops | bytes accessed | tf_op | source)
XLA Modules:
  0.0 128.6 jit_solution(13374842650373584348)
XLA Ops:
  0.0 126.7 %moe_layer.1 = bf16[128,2048]{1,0:T(8,128)(2,1)} custom-call(bf16[128,2048]{1,0:T(8,128)(2,1)} %tokens_in.1, f32[1,2048]{1,0:T(1,128)} %bitcast.14, s32[6,128]{1,0:T(8,128)} %bitcast.15, s32[6,128]{1,0:T(8,128)} %bitcast.16, f32[6,128]{1,0:T(8,128)} %bitcast.17, bf16[2,176,2048]{2,1,0:T(8,128)(2,1)} %bitcast.9, bf16[2,176,2048]{2,1,0:T(8,128)(2,1)} %bitcast.10, ...), custom_call_target="tpu_custom_call" | custom-call | tf_op jit(solution)/shard_map/moe_layer/pallas_call | solution.py:754
  126.7 1.9 %copy.13 = bf16[128,2048]{1,0:T(8,128)(2,1)} copy(bf16[128,2048]{1,0:T(8,128)(2,1)} %moe_layer.1) | data formatting | bytes 1048576

commit v3 on v2

--- a/solution.py
+++ b/solution.py
@@ -205,8 +205,8 @@
         copy_to(source, place(2), far_send.at[group(k)], far_recv.at[k], across)
         for k, (source, place) in enumerate(chunks)
     ]
-    late = range(first_down + 2, n)
-    for k in [*range(first_down - 1), first_down, first_down - 1, first_down + 1]:
+    late = range(first_down + 3, n)
+    for k in [*range(first_down - 1), first_down, first_down - 1, first_down + 1, first_down + 2]:
         far[k].start()
 
     @pl.when(core == 0)
@@ -511,11 +511,16 @@
 
         @pl.when(at_end == 1)
         def _():
-            for r, slot in ((3, 0), (2, 2), (1, 1)):
+            for r, slot in ((3, 0), (2, 2)):
                 if c == end:
                     side_leg(c, r).wait_recv()
                 block(c, r)
-                leg(c, r, slot, 1, join_sem(c, slot) if r > 1 else last_sem(c)).start()
+                leg(c, r, slot, 1, join_sem(c, slot)).start()
+            if c == end:
+                side_leg(c, 1).wait_recv()
+            for k in {end - 1: (), end: (end - 1, end)}.get(c, (c,)):
+                block(k, 1)
+                leg(k, 1, 1, 1, last_sem(k)).start()
 
         @pl.when(inner)
         def _():
@@ -646,15 +651,15 @@
         for step in steps.get(c, []):
             step()
 
+    turn(end - 1)
     share_far.wait_recv()
     share_on = remote(sb.at[2], sb.at[3], t_send, t_recv.at[2], mate)
+    join(6)
     sh[2] = shared_act(sb[2])
     remote(sh.at[2], whid.at[2], h_send, h_recv.at[1], across)
     share_on.wait_recv()
     sh[3] = shared_act(sb[3])
     remote(sh.at[3], whid.at[3], h_send, h_recv.at[1], diagonal)
-    join(6)
-    turn(end - 1)
     join(7)
     turn(end)
     for c in range(end - 2, end + 1):

time: 129 us -> 129 us (level)
  no operation moved by 1% of the time
where the time goes in v3:
time: 129 us
  Pallas kernels  127 us (98%)
  local copies, waits for them, and re-layouts  1.88 us (1%)
    pallas_call x1, Pallas kernels, fused(): pl.pallas_call(functools.partial(layer_kernel, n_rows_z), out_shape=jax.S...  127 us

profile of v3, /device:TPU:0, one launch (start us, length us, event | category | flops | bytes accessed | tf_op | source)
XLA Modules:
  0.0 129.1 jit_solution(18337097219590310720)
XLA Ops:
  0.0 127.2 %moe_layer.1 = bf16[128,2048]{1,0:T(8,128)(2,1)} custom-call(bf16[128,2048]{1,0:T(8,128)(2,1)} %tokens_in.1, f32[1,2048]{1,0:T(1,128)} %bitcast.14, s32[6,128]{1,0:T(8,128)} %bitcast.15, s32[6,128]{1,0:T(8,128)} %bitcast.16, f32[6,128]{1,0:T(8,128)} %bitcast.17, bf16[2,176,2048]{2,1,0:T(8,128)(2,1)} %bitcast.9, bf16[2,176,2048]{2,1,0:T(8,128)(2,1)} %bitcast.10, ...), custom_call_target="tpu_custom_call" | custom-call | tf_op jit(solution)/shard_map/moe_layer/pallas_call | solution.py:759
  127.2 1.9 %copy.13 = bf16[128,2048]{1,0:T(8,128)(2,1)} copy(bf16[128,2048]{1,0:T(8,128)(2,1)} %moe_layer.1) | data formatting | bytes 1048576
